TPU v7x, 32 devices: a whole 2x2x4 slice. The times are simulated.
32 devices in a mesh: row: 8 (over y, x, core), col: 4 (over z).
Axes of the slice: x: 2, y: 2, z: 4, core: 2. Of those that a mesh axis runs over, the one named last changes fastest.
Arguments:
- band_tiles: bfloat16 [8, 64, 256, 256], P('row', 'col'), may hold values from 0.0009994507 to 1
- band_cell: int32 [8, 64], P('row', 'col'), may hold values from 0 to 63, as said below
- band_count: int32 [8, 4], P('row', 'col'), may hold values from 1 to 16, as said below
- matrix_tiles: bfloat16 [8, 64, 256, 256], P('row', 'col'), may hold values from 7.390976e-05 to 0.07421875
- matrix_col: int32 [8, 64], P('row', 'col'), may hold values from 0 to 31
- matrix_live: int32 [8, 64], P('row', 'col'), may hold values 0 or 1
Outputs:
- reached: bfloat16 [4096, 32768], P('row', 'col')
- gained: float32 [], replicated
Inputs may be any that keep to these rules, and one draw needn't show every extreme that they name: The band_cell values of one device's 16 slots are distinct. `band_count`: among the 4 devices of one index of row, the live slots with slot number 16 // 2 or more number at most 8 in all.
All inputs are finite; a program needn't handle non-finite values. No bound on the sum of `matrix_live` on one device may be relied on, other than what follows from the above.
Results may differ from a plain program's by a relative error of at most 0.001.
Values may be sent and summed in bfloat16 or wider, within the bound.
No kernel may reach another device: no remote copies, remote signals or barrier semaphores. Data moves between devices by JAX's collectives and lax.ppermute only.
A program may use at most 128 MiB of HBM per device.

v0:
```python
import jax
import jax.numpy as jnp
from jax import lax
from jax.sharding import PartitionSpec as P

TILES = 128
BR = 2


def on_device(band_tiles, band_cell, band_count, matrix_tiles, matrix_col, matrix_live):
    slots_own = band_tiles.shape[1]
    tile = band_tiles.shape[-1]
    n_col = lax.axis_size("col")
    tcols = TILES // n_col
    places = BR * tcols
    spots = jnp.arange(places, dtype=jnp.int32)
    b_tiles, b_index, b_live = (
        lax.all_gather(matrix_tiles, "row", axis=0, tiled=True),
        lax.all_gather(matrix_col, "row", axis=0, tiled=True),
        lax.all_gather(matrix_live, "row", axis=0, tiled=True),
    )
    flat_tiles = b_tiles.reshape(-1, tile, tile)
    half = slots_own // 2
    front_tiles, a_cell, a_count = (
        lax.all_gather(band_tiles[:, :half], "col", axis=1, tiled=True),
        lax.all_gather(band_cell, "col", axis=1, tiled=True),
        lax.all_gather(band_count, "col", axis=1, tiled=True),
    )
    counts = a_count[0]
    spill = jnp.maximum(counts - half, 0)
    before = jnp.cumsum(spill) - spill
    ending = before + spill
    mine = lax.axis_index("col")
    own_before = jnp.take(before, mine)
    own_spill = jnp.maximum(band_count[0, 0] - half, 0)
    pack_spot = jnp.arange(half, dtype=jnp.int32)
    upper = jnp.arange(half, dtype=jnp.int32)
    place_w = (
        (pack_spot[:, None] == own_before + upper[None, :]) & (upper[None, :] < own_spill)
    ).astype(jnp.bfloat16)
    packed = jnp.einsum(
        "qs,sxy->qxy", place_w, band_tiles[0, half:], preferred_element_type=jnp.float32
    )
    spilled = lax.psum(packed.astype(jnp.bfloat16), "col")
    holder = jnp.sum((ending[None, :] <= pack_spot[:, None]).astype(jnp.int32), axis=1)
    holder = jnp.clip(holder, 0, n_col - 1)
    spill_slot = jnp.clip(half + pack_spot - jnp.take(before, holder), 0, slots_own - 1)
    spill_cell = jnp.take(a_cell[0], holder * slots_own + spill_slot)
    spill_valid = pack_spot < jnp.sum(spill)
    front = jnp.arange(n_col * half, dtype=jnp.int32)
    front_source = front // half
    front_slot = front % half
    front_cell = jnp.take(a_cell[0], front_source * slots_own + front_slot)
    front_valid = front_slot < jnp.take(counts, front_source)
    sources = jnp.concatenate([front_source, holder])
    cells = jnp.concatenate([front_cell, spill_cell])
    valid = jnp.concatenate([front_valid, spill_valid])
    tiles = jnp.concatenate([front_tiles[0], spilled], axis=0)
    k_glob = sources * tcols + cells % tcols
    i_loc = cells // tcols
    picked = jnp.take(flat_tiles, k_glob, axis=0)
    picked_index = jnp.take(b_index.reshape(-1), k_glob)
    picked_live = jnp.take(b_live.reshape(-1), k_glob)
    live = (picked_live > 0) & valid
    position = i_loc * tcols + picked_index
    product = jnp.einsum("axy,ayz->axz", tiles, picked, preferred_element_type=jnp.float32)
    weights = ((position[:, None] == spots[None, :]) & live[:, None]).astype(jnp.float32)
    summed = jnp.einsum("ap,axz->pxz", weights, product, precision=lax.Precision.HIGHEST)
    own_live = jnp.arange(slots_own, dtype=jnp.int32) < band_count[0, 0]
    own_w = ((band_cell[0][:, None] == spots[None, :]) & own_live[:, None]).astype(jnp.bfloat16)
    base = jnp.einsum("sp,sxz->pxz", own_w, band_tiles[0], preferred_element_type=jnp.float32)
    expanded = jnp.minimum(1.0, base + summed)
    block = (
        expanded.reshape(BR, tcols, tile, tile)
        .transpose(0, 2, 1, 3)
        .reshape(BR * tile, tcols * tile)
    )
    total = lax.psum(jnp.sum(expanded - base), ("row", "col"))
    devices = lax.axis_size("row") * n_col
    gained = total / (tile * tile * devices * places)
    return (block.astype(jnp.bfloat16), gained)


def solution(mesh):
    in_specs = (
        P("row", "col", None, None),
        P("row", "col"),
        P("row", "col"),
        P("row", "col", None, None),
        P("row", "col"),
        P("row", "col"),
    )
    out_specs = (P("row", "col"), P())
    return jax.shard_map(
        on_device, mesh=mesh, in_specs=in_specs, out_specs=out_specs, check_vma=False
    )
```

profile of v0, /device:TPU:0, one launch (start us, length us, event | category | flops | bytes accessed | tf_op | source)
XLA Modules:
  0.0 310.5 jit_solution(6108352041416000376)
XLA Ops:
  8.0 0.0 copy-start
  8.0 0.0 all-reduce.5.cloned.1.call-start
  8.9 1.2 dynamic-slice.3
  10.8 0.7 bitcast_dynamic-update-slice_fusion
  11.5 0.8 bitcast_dynamic-update-slice_fusion.1
  12.2 9.9 %all-reduce.2 = (s32[4]{0:T(128)S(1)}, s32[64]{0:T(128)S(1)}) all-reduce(s32[4]{0:T(128)S(1)} %bitcast_dynamic-update-slice_fusion, s32[64]{0:T(128)S(1)} %bitcast_dynamic-update-slice_fusion.1), channel_id=1, replica_groups=mesh['row'=8,'col'=4] {'col'}, use_global_device_ids=true, to_apply=%add.1 | all-reduce | flops 68 | bytes 544
  22.1 0.6 fusion.42
  22.8 0.2 reduce-window.8
  23.0 0.6 dynamic-slice.2
  24.2 1.3 slice.7
  25.5 0.0 copy-start.2
  25.5 0.0 copy-start.3
  25.5 1.7 convolution_convert_fusion
  27.2 0.0 all-reduce.5.cloned.1.call-update
  27.2 0.0 all-gather.7.cloned.1.call-start
  27.3 0.5 all-gather.7.cloned.1.call-update
  27.8 0.0 all-gather.5.cloned.1.call-start
  27.9 0.0 copy-done
  27.9 1.1 slice.35
  28.9 0.0 all-gather.5.cloned.1.call-update
  29.0 0.1 convert_reduce_fusion
  29.1 0.6 gather_fusion.1
  29.8 0.6 gather_fusion.2
  30.4 0.7 gather_fusion
  31.1 0.0 copy-done.2
  31.1 8.8 %all-gather = s32[8,1,16]{2,1,0:T(1,128)S(1)} all-gather(s32[1,1,16]{2,1,0:T(1,128)S(1)} %bitcast.89), channel_id=1, replica_groups=mesh['row'=8,'col'=4] {'row'}, dimensions={0}, use_global_device_ids=true | all-gather | bytes 576 | tf_op jit(solution)/shard_map/all_gather | solution.py:19
  39.9 0.5 broadcast.1045
  40.4 0.7 reduce.7
  41.1 0.1 reshape.379
  41.2 0.0 copy-done.3
  41.2 9.2 %all-gather.1 = s32[8,1,16]{2,1,0:T(1,128)S(1)} all-gather(s32[1,1,16]{2,1,0:T(1,128)S(1)} %bitcast.90), channel_id=1, replica_groups=mesh['row'=8,'col'=4] {'row'}, dimensions={0}, use_global_device_ids=true | all-gather | bytes 576 | tf_op jit(solution)/shard_map/all_gather | solution.py:20
  50.4 0.7 reduce.8
  51.1 0.1 reshape.380
  51.2 0.1 compare_and_fusion
  51.3 0.8 gather_fusion.4
  52.1 0.8 gather_fusion.5
  52.9 0.6 iota_compare_fusion.5
  53.4 0.6 fusion.45
  54.1 2.5 fusion.32
  56.6 0.1 fusion.37
  56.7 0.1 select_add_fusion
  56.8 0.1 add_and_fusion
  56.8 21.7 %all-reduce.5.cloned.1.call-done = bf16[8,256,256]{2,0,1:T(8,128)(2,1)} async-done(((bf16[8,256,256]{2,0,1:T(8,128)(2,1)}), bf16[8,256,256]{2,0,1:T(8,128)(2,1)}) %all-reduce.5.cloned.1.call-update) | async-done | bytes 1048592 | tf_op jit(solution)/shard_map/psum | solution.py:44
  78.5 1.4 copy.21
  79.9 38.5 %all-gather.7.cloned.1.call-done = bf16[8,16,256,256]{3,2,1,0:T(8,128)(2,1)} async-done(((bf16[1,16,256,256]{3,2,1,0:T(8,128)(2,1)}), bf16[8,16,256,256]{3,2,1,0:T(8,128)(2,1)}) %all-gather.7.cloned.1.call-update) | async-done | bytes 16777232 | tf_op jit(solution)/shard_map/all_gather | solution.py:18
  118.5 10.4 %gather_fusion.3 = bf16[40,256,256]{2,1,0:T(8,128)(2,1)} fusion(bf16[128,256,256]{2,1,0:T(8,128)(2,1)} %bitcast.85, s32[1024]{0:T(1024)S(1)} %pad_clamp_fusion), kind=kCustom, calls=%fused_computation.5 | custom fusion | bytes 10485920 | tf_op jit(solution)/shard_map/jit(_take)/gather | solution.py:61
  128.9 71.6 %all-gather.5.cloned.1.call-done = bf16[1,32,256,256]{3,2,0,1:T(8,128)(2,1)} async-done(((bf16[1,8,256,256]{3,2,0,1:T(8,128)(2,1)}), bf16[1,32,256,256]{3,2,0,1:T(8,128)(2,1)}) %all-gather.5.cloned.1.call-update) | async-done | bytes 4194320 | tf_op jit(solution)/shard_map/all_gather | solution.py:25
  200.6 9.5 %fusion.3 = f32[40,256,256]{2,1,0:T(8,128)} fusion(bf16[8,256,256]{2,1,0:T(8,128)(2,1)S(1)} %copy.21, bf16[32,256,256]{2,1,0:T(8,128)(2,1)} %bitcast.91, bf16[40,256,256]{2,1,0:T(8,128)(2,1)} %gather_fusion.3, pred[40]{0:T(512)(128)(4,1)S(1)} %get-tuple-element.16), kind=kOutput, calls=%fused_computation.11 | convolution fusion | flops 1347420160 | bytes 20971560 | tf_op jit(solution)/shard_map/axy,ayz->axz/dot_general | solution.py:66
  210.0 0.0 copy-start.1
  210.0 18.0 %fusion.1 = f32[64,256,256]{2,0,1:T(8,128)S(1)} fusion(f32[40,256,256]{2,1,0:T(8,128)} %fusion.3, s32[40]{0:T(128)S(1)} %select_add_fusion, pred[40]{0:T(512)(128)(4,1)S(1)} %add_and_fusion), kind=kOutput, calls=%fused_computation.9 | convolution fusion | flops 2013271040 | bytes 27263176 | tf_op jit(solution)/shard_map/ap,axz->pxz/dot_general | solution.py:68
  228.1 0.0 copy-done.1
  228.1 9.9 %subtract_reduce_fusion = (f32[]{:T(128)}, bf16[64,256,256]{2,0,1:T(8,128)(2,1)}) fusion(f32[64,256,256]{2,0,1:T(8,128)S(1)} %fusion.1, bf16[16,256,256]{2,1,0:T(8,128)(2,1)S(1)} %bitcast.83, s32[16]{0:T(128)S(1)} %bitcast.88, pred[16]{0:T(512)(128)(4,1)S(1)} %iota_compare_fusion.6), kind=kOutput, calls=%fused_computation.6 | convolution fusion | flops 155191296 | bytes 27263060 | tf_op jit(solution)/shard_map/sp,sxz->pxz/dot_general | solution.py:71
  238.0 38.9 %psum.15 = f32[]{:T(128)} all-reduce(f32[]{:T(128)} %get-tuple-element.18), channel_id=1, replica_groups=mesh['row'=8,'col'=4] {'row','col'}, use_global_device_ids=true, to_apply=%region_5.7 | all-reduce | flops 1 | bytes 8 | tf_op jit(solution)/shard_map/psum | solution.py:78
  276.9 7.8 %copy.23 = bf16[2,256,32,256]{3,2,1,0:T(8,128)(2,1)} copy(bf16[2,256,32,256]{3,2,0,1:T(8,128)(2,1)} %bitcast.80) | data formatting | bytes 16777216 | tf_op jit(solution)/shard_map/convert_element_type | solution.py:81
  284.7 16.6 %copy.25 = bf16[64,8,32,256]{3,1,2,0:T(8,128)(2,1)} copy(bf16[64,8,32,256]{3,2,1,0:T(8,128)(2,1)} %bitcast.81) | data formatting | bytes 16777216
  (19 shorter events, 0.1 us)
Async XLA Ops:
  8.0 19.9 %copy-start = (bf16[1,16,256,256]{3,2,1,0:T(8,128)(2,1)S(1)}, bf16[1,16,256,256]{3,2,1,0:T(8,128)(2,1)}, u32[]{:S(2)}) copy-start(bf16[1,16,256,256]{3,2,1,0:T(8,128)(2,1)} %param.8) | copy-start | bytes 6291460
  8.0 70.5 %all-reduce.5.cloned.1.call-start = ((), (), s32[]{:S(2)}) async-start(), calls=%async_computation.1 | async-start | bytes 2097152 | tf_op jit(solution)/shard_map/psum | solution.py:44
  25.5 5.6 %copy-start.2 = (s32[1,16]{1,0:T(1,128)S(1)}, s32[1,16]{1,0:T(1,128)}, u32[]{:S(2)}) copy-start(s32[1,16]{1,0:T(1,128)} %param.12) | copy-start | bytes 196
  25.5 15.7 %copy-start.3 = (s32[1,16]{1,0:T(1,128)S(1)}, s32[1,16]{1,0:T(1,128)}, u32[]{:S(2)}) copy-start(s32[1,16]{1,0:T(1,128)} %param.13) | copy-start | bytes 196
  27.2 91.3 %all-gather.7.cloned.1.call-start = ((), (), s32[]{:S(2)}) async-start(), calls=%async_computation.2 | async-start | bytes 18874368 | tf_op jit(solution)/shard_map/all_gather | solution.py:18
  27.8 172.7 %all-gather.5.cloned.1.call-start = ((), (), s32[]{:S(2)}) async-start(), calls=%async_computation | async-start | bytes 5242880 | tf_op jit(solution)/shard_map/all_gather | solution.py:25
  210.0 18.0 %copy-start.1 = (s32[1,16]{1,0:T(1,128)S(1)}, s32[1,16]{1,0:T(1,128)}, u32[]{:S(2)}) copy-start(s32[1,16]{1,0:T(1,128)} %param.9) | copy-start | bytes 196
Sparse Core Ops, SparseCore 0:
  27.3 51.1 all-reduce.4
Sparse Core Ops, SparseCore 1:
  29.6 88.8 all-gather.6
  119.9 80.6 all-gather.4
where the time goes:
time: 311 us
  waiting for transfers between devices  132 us (42%)
  blocking collectives  66.8 us (21%)
  local copies, waits for them, and re-layouts  46.8 us (15%)
  matrix products  39.1 us (13%)
  between operations  19.5 us (6%)
  other arithmetic  5.76 us (2%)
    all_gather x1, waiting for transfers between devices, on_device(): lax.all_gather(band_tiles[:, :half], 'col', axis=1, tiled=True)  71.6 us
    psum x1, blocking collectives, on_device(): total = lax.psum(jnp.sum(expanded - base), ('row', 'col'))  38.9 us
    all_gather x1, waiting for transfers between devices, on_device(): lax.all_gather(matrix_tiles, 'row', axis=0, tiled=True)  38.5 us
    psum x1, waiting for transfers between devices, on_device(): spilled = lax.psum(packed.astype(jnp.bfloat16), 'col')  21.7 us
    unnamed x14, local copies, waits for them, and re-layouts  19.3 us
    dot_general x1, matrix products, on_device(): jnp.einsum('ap,axz->pxz', weights, product, precision=lax.Precision.HIGHEST)  18 us
    gather x1, local copies, waits for them, and re-layouts, on_device(): picked = jnp.take(flat_tiles, k_glob, axis=0)  10.4 us
    dot_general x1, matrix products, on_device(): jnp.einsum('sp,sxz->pxz', own_w, band_tiles[0], preferred_element_type=jn...  9.92 us
  transfers between devices with their start and end apart: 3, of which 3 were waited for; matrix products, arithmetic and copies ran while one was open for 7% of the time, Pallas kernels for 0%

commit v1 on v0

--- a/solution.py
+++ b/solution.py
@@ -41,7 +41,7 @@
     packed = jnp.einsum(
         "qs,sxy->qxy", place_w, band_tiles[0, half:], preferred_element_type=jnp.float32
     )
-    spilled = lax.psum(packed.astype(jnp.bfloat16), "col")
+    spilled = jnp.sum(lax.all_gather(packed.astype(jnp.bfloat16), "col"), axis=0)
     holder = jnp.sum((ending[None, :] <= pack_spot[:, None]).astype(jnp.int32), axis=1)
     holder = jnp.clip(holder, 0, n_col - 1)
     spill_slot = jnp.clip(half + pack_spot - jnp.take(before, holder), 0, slots_own - 1)

time: 311 us -> 388 us (1.25)
  waiting for transfers between devices: 132 us -> 209 us
    all_gather x0 -> x1, waiting for transfers between devices: none -> 50.3 us  [on_device(): lax.all_gather(packed.astype(jnp.bfloat16), 'col')]
    all_gather x1, waiting for transfers between devices: 38.5 us -> 86.1 us  [on_device(): lax.all_gather(matrix_tiles, 'row', axis=0, tiled=True)]
    psum x1 -> x0, waiting for transfers between devices: 21.7 us -> none  [on_device(): spilled = lax.psum(packed.astype(jnp.bfloat16), 'col')]
where the time goes in v1:
time: 388 us; the launch traced here: 387 us
  waiting for transfers between devices  209 us (54%)
  blocking collectives  66.4 us (17%)
  local copies, waits for them, and re-layouts  45.8 us (12%)
  matrix products  38.9 us (10%)
  between operations  17.8 us (5%)
  other arithmetic  9.6 us (2%)
    all_gather x1, waiting for transfers between devices, on_device(): lax.all_gather(matrix_tiles, 'row', axis=0, tiled=True)  86.1 us
    all_gather x1, waiting for transfers between devices, on_device(): lax.all_gather(band_tiles[:, :half], 'col', axis=1, tiled=True)  71.7 us
    all_gather x1, waiting for transfers between devices, on_device(): lax.all_gather(packed.astype(jnp.bfloat16), 'col')  50.3 us
    psum x1, blocking collectives, on_device(): total = lax.psum(jnp.sum(expanded - base), ('row', 'col'))  39 us
    unnamed x14, local copies, waits for them, and re-layouts  19.3 us
    dot_general x1, matrix products, on_device(): jnp.einsum('ap,axz->pxz', weights, product, precision=lax.Precision.HIGHEST)  18 us
    gather x1, local copies, waits for them, and re-layouts, on_device(): picked = jnp.take(flat_tiles, k_glob, axis=0)  10.6 us
    unnamed x1, blocking collectives  9.92 us
  transfers between devices with their start and end apart: 3, of which 3 were waited for; matrix products, arithmetic and copies ran while one was open for 7% of the time, Pallas kernels for 0%

profile of v1, /device:TPU:0, one launch (start us, length us, event | category | flops | bytes accessed | tf_op | source)
XLA Modules:
  0.0 387.5 jit_solution(2758489327493369942)
XLA Ops:
  7.2 0.0 copy-start
  7.2 0.0 all-gather.11.cloned.1.call-start
  8.0 1.2 dynamic-slice.3
  9.9 0.7 bitcast_dynamic-update-slice_fusion
  10.6 0.8 bitcast_dynamic-update-slice_fusion.1
  11.4 9.9 %all-reduce.2 = (s32[4]{0:T(128)S(1)}, s32[64]{0:T(128)S(1)}) all-reduce(s32[4]{0:T(128)S(1)} %bitcast_dynamic-update-slice_fusion, s32[64]{0:T(128)S(1)} %bitcast_dynamic-update-slice_fusion.1), channel_id=1, replica_groups=mesh['row'=8,'col'=4] {'col'}, use_global_device_ids=true, to_apply=%add.1 | all-reduce | flops 68 | bytes 544
  21.3 0.7 fusion.42
  22.0 0.2 reduce-window.8
  22.2 0.6 dynamic-slice.2
  23.4 1.3 slice.7
  24.7 0.0 copy-start.2
  24.7 0.0 copy-start.3
  24.7 1.7 convolution_convert_fusion
  26.4 0.0 all-gather.11.cloned.1.call-update
  26.4 0.0 all-gather.9.cloned.1.call-start
  26.5 0.7 all-gather.9.cloned.1.call-update
  27.2 0.0 all-gather.7.cloned.1.call-start
  27.2 0.0 copy-done
  27.3 1.1 slice.35
  28.4 0.0 all-gather.7.cloned.1.call-update
  28.4 0.1 convert_reduce_fusion
  28.5 0.6 gather_fusion.1
  29.2 0.6 gather_fusion.2
  29.9 0.7 gather_fusion
  30.6 0.0 copy-done.2
  30.6 8.8 %all-gather.1 = s32[8,1,16]{2,1,0:T(1,128)S(1)} all-gather(s32[1,1,16]{2,1,0:T(1,128)S(1)} %bitcast.91), channel_id=1, replica_groups=mesh['row'=8,'col'=4] {'row'}, dimensions={0}, use_global_device_ids=true | all-gather | bytes 576 | tf_op jit(solution)/shard_map/all_gather | solution.py:19
  39.4 0.5 broadcast.1045
  39.9 0.7 reduce.8
  40.6 0.1 reshape.379
  40.6 0.0 copy-done.3
  40.6 8.8 %all-gather.2 = s32[8,1,16]{2,1,0:T(1,128)S(1)} all-gather(s32[1,1,16]{2,1,0:T(1,128)S(1)} %bitcast.92), channel_id=1, replica_groups=mesh['row'=8,'col'=4] {'row'}, dimensions={0}, use_global_device_ids=true | all-gather | bytes 576 | tf_op jit(solution)/shard_map/all_gather | solution.py:20
  49.4 0.7 reduce.9
  50.1 0.1 reshape.380
  50.2 0.1 compare_and_fusion
  50.3 0.8 gather_fusion.4
  51.1 0.8 gather_fusion.5
  51.8 0.6 iota_compare_fusion.5
  52.5 0.7 fusion.45
  53.2 2.7 fusion.32
  55.8 0.1 fusion.37
  55.9 0.1 select_add_fusion
  56.0 0.1 add_and_fusion
  56.1 50.3 %all-gather.11.cloned.1.call-done = bf16[32,256,256]{2,0,1:T(8,128)(2,1)} async-done(((bf16[8,256,256]{2,0,1:T(8,128)(2,1)}), bf16[32,256,256]{2,0,1:T(8,128)(2,1)}) %all-gather.11.cloned.1.call-update) | async-done | bytes 4194320 | tf_op jit(solution)/shard_map/all_gather | solution.py:44
  106.4 3.6 bitcast_reduce_fusion
  109.9 0.2 copy.23
  110.1 86.1 %all-gather.9.cloned.1.call-done = bf16[8,16,256,256]{3,2,1,0:T(8,128)(2,1)} async-done(((bf16[1,16,256,256]{3,2,1,0:T(8,128)(2,1)}), bf16[8,16,256,256]{3,2,1,0:T(8,128)(2,1)}) %all-gather.9.cloned.1.call-update) | async-done | bytes 16777232 | tf_op jit(solution)/shard_map/all_gather | solution.py:18
  196.2 10.6 %gather_fusion.3 = bf16[40,256,256]{2,1,0:T(8,128)(2,1)} fusion(bf16[128,256,256]{2,1,0:T(8,128)(2,1)} %bitcast.87, s32[1024]{0:T(1024)S(1)} %pad_clamp_fusion), kind=kCustom, calls=%fused_computation.5 | custom fusion | bytes 10485920 | tf_op jit(solution)/shard_map/jit(_take)/gather | solution.py:61
  206.8 71.7 %all-gather.7.cloned.1.call-done = bf16[1,32,256,256]{3,2,0,1:T(8,128)(2,1)} async-done(((bf16[1,8,256,256]{3,2,0,1:T(8,128)(2,1)}), bf16[1,32,256,256]{3,2,0,1:T(8,128)(2,1)}) %all-gather.7.cloned.1.call-update) | async-done | bytes 4194320 | tf_op jit(solution)/shard_map/all_gather | solution.py:25
  278.5 9.5 %fusion.3 = f32[40,256,256]{2,1,0:T(8,128)} fusion(bf16[8,256,256]{2,1,0:T(8,128)(2,1)S(1)} %copy.23, bf16[32,256,256]{2,1,0:T(8,128)(2,1)} %bitcast.93, bf16[40,256,256]{2,1,0:T(8,128)(2,1)} %gather_fusion.3, pred[40]{0:T(512)(128)(4,1)S(1)} %get-tuple-element.16), kind=kOutput, calls=%fused_computation.11 | convolution fusion | flops 1347420160 | bytes 20971560 | tf_op jit(solution)/shard_map/axy,ayz->axz/dot_general | solution.py:66
  288.0 0.0 copy-start.1
  288.0 18.0 %fusion.1 = f32[64,256,256]{2,0,1:T(8,128)S(1)} fusion(f32[40,256,256]{2,1,0:T(8,128)} %fusion.3, s32[40]{0:T(128)S(1)} %select_add_fusion, pred[40]{0:T(512)(128)(4,1)S(1)} %add_and_fusion), kind=kOutput, calls=%fused_computation.9 | convolution fusion | flops 2013271040 | bytes 27263176 | tf_op jit(solution)/shard_map/ap,axz->pxz/dot_general | solution.py:68
  306.1 0.0 copy-done.1
  306.1 9.7 %subtract_reduce_fusion = (f32[]{:T(128)}, bf16[64,256,256]{2,0,1:T(8,128)(2,1)}) fusion(f32[64,256,256]{2,0,1:T(8,128)S(1)} %fusion.1, bf16[16,256,256]{2,1,0:T(8,128)(2,1)S(1)} %bitcast.85, s32[16]{0:T(128)S(1)} %bitcast.90, pred[16]{0:T(512)(128)(4,1)S(1)} %iota_compare_fusion.6), kind=kOutput, calls=%fused_computation.6 | convolution fusion | flops 155191296 | bytes 27263060 | tf_op jit(solution)/shard_map/sp,sxz->pxz/dot_general | solution.py:71
  315.8 39.0 %psum.7 = f32[]{:T(128)} all-reduce(f32[]{:T(128)} %get-tuple-element.18), channel_id=1, replica_groups=mesh['row'=8,'col'=4] {'row','col'}, use_global_device_ids=true, to_apply=%region_5.7 | all-reduce | flops 1 | bytes 8 | tf_op jit(solution)/shard_map/psum | solution.py:78
  354.7 7.8 %copy.25 = bf16[2,256,32,256]{3,2,1,0:T(8,128)(2,1)} copy(bf16[2,256,32,256]{3,2,0,1:T(8,128)(2,1)} %bitcast.82) | data formatting | bytes 16777216 | tf_op jit(solution)/shard_map/convert_element_type | solution.py:81
  362.6 16.6 %copy.27 = bf16[64,8,32,256]{3,1,2,0:T(8,128)(2,1)} copy(bf16[64,8,32,256]{3,2,1,0:T(8,128)(2,1)} %bitcast.83) | data formatting | bytes 16777216
  (19 shorter events, 0.1 us)
Async XLA Ops:
  7.2 20.1 %copy-start = (bf16[1,16,256,256]{3,2,1,0:T(8,128)(2,1)S(1)}, bf16[1,16,256,256]{3,2,1,0:T(8,128)(2,1)}, u32[]{:S(2)}) copy-start(bf16[1,16,256,256]{3,2,1,0:T(8,128)(2,1)} %param.8) | copy-start | bytes 6291460
  7.2 99.2 %all-gather.11.cloned.1.call-start = ((), (), s32[]{:S(2)}) async-start(), calls=%async_computation.2 | async-start | bytes 5242880 | tf_op jit(solution)/shard_map/all_gather | solution.py:44
  24.7 5.9 %copy-start.2 = (s32[1,16]{1,0:T(1,128)S(1)}, s32[1,16]{1,0:T(1,128)}, u32[]{:S(2)}) copy-start(s32[1,16]{1,0:T(1,128)} %param.12) | copy-start | bytes 196
  24.7 15.9 %copy-start.3 = (s32[1,16]{1,0:T(1,128)S(1)}, s32[1,16]{1,0:T(1,128)}, u32[]{:S(2)}) copy-start(s32[1,16]{1,0:T(1,128)} %param.13) | copy-start | bytes 196
  26.4 169.8 %all-gather.9.cloned.1.call-start = ((), (), s32[]{:S(2)}) async-start(), calls=%async_computation.1 | async-start | bytes 18874368 | tf_op jit(solution)/shard_map/all_gather | solution.py:18
  27.2 251.3 %all-gather.7.cloned.1.call-start = ((), (), s32[]{:S(2)}) async-start(), calls=%async_computation | async-start | bytes 5242880 | tf_op jit(solution)/shard_map/all_gather | solution.py:25
  288.0 18.0 %copy-start.1 = (s32[1,16]{1,0:T(1,128)S(1)}, s32[1,16]{1,0:T(1,128)}, u32[]{:S(2)}) copy-start(s32[1,16]{1,0:T(1,128)} %param.9) | copy-start | bytes 196
Sparse Core Ops, SparseCore 0:
  26.6 79.7 all-gather.10
  108.2 87.9 all-gather.8
  197.8 80.7 all-gather.6
